TPU v7x, 512 devices: a whole 4x4x16 slice. The times are simulated.
512 devices in a mesh: group: 16 (over y, x), member: 32 (over z, core).
Axes of the slice: x: 4, y: 4, z: 16, core: 2. Of those that a mesh axis runs over, the one named last changes fastest.
Arguments:
- tokens: bfloat16 [65536, 2048], P(('group', 'member')), may hold values from -6 to 6
- cotangent: bfloat16 [65536, 2048], P(('group', 'member')), may hold values from -6 to 6
- w_gate: bfloat16 [2048, 512], P('member'), may hold values from -0.125 to 0.125
- w_up: bfloat16 [2048, 512], P('member'), may hold values from -0.125 to 0.125
- w_down: bfloat16 [2048, 512], P('member'), may hold values from -0.125 to 0.125
- basis: float32 [2048, 256], P('member'), may hold values from -0.088388348 to 0.088388348
- first_moment: float32 [3, 256, 512], P(None, 'member'), may hold values from -3 to 3
- second_moment: float32 [3, 256, 512], P(None, 'member'), may hold values from 0.1 to 2
Outputs:
- input_grad: bfloat16 [65536, 2048], P(('group', 'member'))
- new_first: float32 [3, 256, 512], P(None, 'member')
- new_second: float32 [3, 256, 512], P(None, 'member')
- updates: float32 [3, 2048, 512], P(None, 'member')
All inputs are finite; a program needn't handle non-finite values.
Results may differ from a plain program's by a relative error of at most 0.008.
Values may be sent and summed in bfloat16 or wider, within the bound.
A program may use at most 64 MiB of HBM per device.

v0:
```python
import math
import jax
import jax.numpy as jnp
from jax import lax
from jax.sharding import Mesh
from jax.sharding import PartitionSpec as P

FF = 512
RANK = 256
MEMBER = ("member_0", "member_1")
GROUP_MEMBER = ("group", "member_0", "member_1")


def in_one_piece(arrays, axis, dim, along):
    both = jnp.concatenate(arrays, axis=along)
    whole, at, gathered = (lax.all_gather(both, axis, axis=dim, tiled=True), 0, [])
    for a in arrays:
        gathered.append(lax.slice_in_dim(whole, at, at + a.shape[along], axis=along))
        at += a.shape[along]
    return tuple(gathered)


def joined_along(pieces, dim):
    pieces = jnp.moveaxis(pieces, 0, dim)
    shape = pieces.shape
    return pieces.reshape(*shape[:dim], shape[dim] * shape[dim + 1], *shape[dim + 2 :])


def copy_for_each(value, axis):
    peers = lax.axis_size(axis)
    return lax.all_to_all(
        jnp.broadcast_to(value[None], (peers, *value.shape)), axis, 0, 0, tiled=True
    )


def gathered_copies(value, axis, dim):
    return joined_along(copy_for_each(value, axis), dim)


def in_blocks(value, dim, peers):
    before, after = (value.shape[:dim], value.shape[dim + 1 :])
    return jnp.moveaxis(value.reshape(*before, peers, -1, *after), dim, 0)


def sum_at_owner(value, axis, dim):
    pieces = in_blocks(value, dim, lax.axis_size(axis))
    arrived = lax.all_to_all(pieces, axis, split_axis=0, concat_axis=0, tiled=True)
    return arrived.sum(axis=0)


def of_everyone(value, axis):
    return copy_for_each(value, axis).sum(axis=0)


def gather_in_order(value, axes, order):
    pieces = value[None]
    for k in order:
        pieces = lax.all_gather(pieces, axes[k], axis=0, tiled=True)
    block = [lax.axis_size(axes[k]) for k in reversed(order)]
    pieces = pieces.reshape(*block, *value.shape)
    turned = sorted(range(len(order)), key=lambda place: order[len(order) - 1 - place])
    return pieces.transpose(*turned, *range(len(order), pieces.ndim)).reshape(-1, *value.shape)


def whole_of(value, axes, order, dim):
    return joined_along(gather_in_order(value, axes, order), dim)


def contract_rows(left, right):
    return lax.dot_general(
        left, right, (((0,), (0,)), ((), ())), preferred_element_type=jnp.float32
    )


def contract_cols(left, right):
    return lax.dot_general(
        left, right, (((1,), (1,)), ((), ())), preferred_element_type=jnp.float32
    )


def split_parts(values):
    high_part = values.astype(jnp.bfloat16)
    low_part = (values - high_part.astype(jnp.float32)).astype(jnp.bfloat16)
    return (high_part, low_part)


def local(tokens, cotangent, w_gate, w_up, w_down, basis, first_moment, second_moment):
    full_gate, full_up, full_down = in_one_piece((w_gate, w_up, w_down), MEMBER, 0, 1)
    gate = jnp.dot(tokens, full_gate, preferred_element_type=jnp.float32)
    up = jnp.dot(tokens, full_up, preferred_element_type=jnp.float32)
    dhid = jnp.dot(cotangent, full_down, preferred_element_type=jnp.float32)
    sig = jax.nn.sigmoid(gate)
    silu = gate * sig
    hidden = (silu * up).astype(jnp.bfloat16)
    dgate = (dhid * up * sig * (1.0 + gate * (1.0 - sig))).astype(jnp.bfloat16)
    dup = (dhid * silu).astype(jnp.bfloat16)
    dx_full = contract_cols(dgate, full_gate) + contract_cols(dup, full_up)
    input_grad = dx_full.astype(jnp.bfloat16)
    full_basis = gathered_copies(basis, MEMBER, 0)
    highest = lax.Precision.HIGHEST
    basis_high, basis_low = split_parts(full_basis)
    x_proj = jnp.dot(tokens, basis_high, preferred_element_type=jnp.float32) + jnp.dot(
        tokens, basis_low, preferred_element_type=jnp.float32
    )
    y_proj = jnp.dot(cotangent, basis_high, preferred_element_type=jnp.float32) + jnp.dot(
        cotangent, basis_low, preferred_element_type=jnp.float32
    )
    x_high, x_low = split_parts(x_proj)
    y_high, y_low = split_parts(y_proj)
    low_gate = contract_rows(x_high, dgate) + contract_rows(x_low, dgate)
    low_up = contract_rows(x_high, dup) + contract_rows(x_low, dup)
    low_down = contract_rows(y_high, hidden) + contract_rows(y_low, hidden)
    local_low = jnp.stack([low_gate, low_up, low_down])
    partial_rows = sum_at_owner(local_low, MEMBER, 1)
    share = of_everyone(partial_rows, "group")
    squares = of_everyone(jnp.sum(share * share), MEMBER)
    limit = math.sqrt(3.0 * RANK * FF)
    factor = jnp.minimum(1.0, limit / jnp.sqrt(squares + 1e-06))
    grad_low = factor * share
    new_first = 0.5 * first_moment + 0.5 * grad_low
    new_second = 0.9 * second_moment + 0.1 * grad_low * grad_low
    step = (new_first / (jnp.sqrt(new_second) + 1e-08)).astype(jnp.bfloat16)
    updates = jnp.einsum(
        "dr,krf->kdf",
        basis,
        whole_of(step, MEMBER, (0, 1), 1).astype(jnp.float32),
        precision=highest,
    )
    return (input_grad, new_first, new_second, updates)


def solution(mesh):
    torus = Mesh(
        mesh.devices.reshape(mesh.shape["group"], 16, 2), ("group", "member_0", "member_1")
    )
    placed = (
        P(GROUP_MEMBER, None),
        P(GROUP_MEMBER, None),
        P(MEMBER, None),
        P(MEMBER, None),
        P(MEMBER, None),
        P(MEMBER, None),
        P(None, MEMBER, None),
        P(None, MEMBER, None),
    )
    return jax.shard_map(
        local,
        mesh=torus,
        in_specs=placed,
        out_specs=(
            P(GROUP_MEMBER, None),
            P(None, MEMBER, None),
            P(None, MEMBER, None),
            P(None, MEMBER, None),
        ),
        check_vma=False,
    )
```

profile of v0, /device:TPU:1, one launch (start us, length us, event | category | flops | bytes accessed | tf_op | source)
XLA Modules:
  0.0 337.4 jit_solution(16014299406178635966)
XLA Ops:
  7.2 1.6 pad_maximum_fusion
  8.9 1.1 broadcast_in_dim.8
  10.0 137.4 %all_to_all.21 = f32[32,64,256]{2,1,0:T(8,128)S(1)} all-to-all(f32[32,64,256]{2,1,0:T(8,128)S(1)} %broadcast_in_dim.8), channel_id=1, replica_groups=mesh['group'=16,'member_0'=16,'member_1'=2] {'member_0','member_1'}, dimensions={0} | all-to-all | bytes 4194304 | tf_op jit(solution)/shard_map/all_to_all | solution.py:31
  147.7 0.8 copy-done.2
  149.1 0.3 fusion.24
  149.8 12.7 %all-gather.3.cloned.1.call-done = bf16[2048,1536]{1,0:T(8,128)(2,1)} async-done(((bf16[64,1536]{1,0:T(8,128)(2,1)}), bf16[2048,1536]{1,0:T(8,128)(2,1)}) %all-gather.3.cloned.1.call-update) | async-done | bytes 6291472 | tf_op jit(solution)/shard_map/all_gather | solution.py:16
  162.4 2.5 fusion.17
  164.9 2.3 fusion.20
  167.3 0.8 multiply_convert_fusion
  169.7 85.5 %all_to_all.22 = f32[32,3,8,512]{3,2,1,0:T(8,128)S(1)} all-to-all(f32[32,3,8,512]{3,2,1,0:T(8,128)S(1)} %maximum_bitcast_fusion), channel_id=1, replica_groups=mesh['group'=16,'member_0'=16,'member_1'=2] {'member_0','member_1'}, dimensions={0} | all-to-all | bytes 3145728 | tf_op jit(solution)/shard_map/all_to_all | solution.py:47
  255.3 1.0 broadcast_in_dim.9
  256.3 6.8 %all-to-all-start.2 = ((f32[16,3,8,512]{3,2,1,0:T(8,128)}), f32[16,3,8,512]{3,2,1,0:T(8,128)S(1)}, u32[]{:S(2)}, u32[]{:S(2)}) async-start(f32[16,3,8,512]{3,2,1,0:T(8,128)} %broadcast_in_dim.9), calls=%async_computation.2 | async-start | bytes 1572864 | tf_op jit(solution)/shard_map/all_to_all | solution.py:31
  263.1 2.4 fusion.4
  265.5 11.0 %all-to-all-done.2 = f32[16,3,8,512]{3,2,1,0:T(8,128)S(1)} async-done(((f32[16,3,8,512]{3,2,1,0:T(8,128)}), f32[16,3,8,512]{3,2,1,0:T(8,128)S(1)}, u32[]{:S(2)}, u32[]{:S(2)}) %all-to-all-start.2) | async-done | bytes 786464 | tf_op jit(solution)/shard_map/all_to_all | solution.py:31
  276.5 0.6 multiply_reduce_fusion
  277.1 1.3 broadcast_in_dim.10
  278.4 5.5 %all-to-all-start.3 = ((f32[32,1,1]{2,1,0:T(1,128)}), f32[32,1,1]{2,1,0:T(1,128)S(1)}, u32[]{:S(2)}, u32[]{:S(2)}) async-start(f32[32,1,1]{2,1,0:T(1,128)} %broadcast_in_dim.10), calls=%async_computation.3 | async-start | bytes 32768 | tf_op jit(solution)/shard_map/all_to_all | solution.py:31
  283.9 3.2 fusion
  287.1 8.6 %all-to-all-done.3 = f32[32,1,1]{2,1,0:T(1,128)S(1)} async-done(((f32[32,1,1]{2,1,0:T(1,128)}), f32[32,1,1]{2,1,0:T(1,128)S(1)}, u32[]{:S(2)}, u32[]{:S(2)}) %all-to-all-start.3) | async-done | bytes 160 | tf_op jit(solution)/shard_map/all_to_all | solution.py:31
  295.8 0.6 reduce_sum.39
  297.1 0.7 divide_convert_fusion
  297.8 21.5 %all-gather = bf16[48,8,512]{2,1,0:T(8,128)(2,1)S(1)} all-gather(bf16[3,8,512]{2,1,0:T(8,128)(2,1)S(1)} %get-tuple-element.4), channel_id=2, replica_groups=mesh['group'=16,'member_0'=16,'member_1'=2] {'member_0'}, dimensions={0}, use_global_device_ids=true | all-gather | bytes 417792 | tf_op jit(solution)/shard_map/all_gather | solution.py:58
  319.2 10.0 %all_gather.11 = bf16[32,3,8,512]{3,2,1,0:T(8,128)(2,1)S(1)} all-gather(bf16[16,3,8,512]{3,2,1,0:T(8,128)(2,1)S(1)} %bitcast.70), channel_id=1, replica_groups=mesh['group'=16,'member_0'=16,'member_1'=2] {'member_1'}, dimensions={0}, use_global_device_ids=true | all-gather | bytes 1179648 | tf_op jit(solution)/shard_map/all_gather | solution.py:58
  329.3 1.3 convolution_bitcast_fusion
  (27 shorter events, 3.2 us)
Async XLA Ops:
  7.2 141.6 %copy-start = (bf16[128,2048]{1,0:T(8,128)(2,1)S(1)}, bf16[128,2048]{1,0:T(8,128)(2,1)}, u32[]{:S(2)}) copy-start(bf16[128,2048]{1,0:T(8,128)(2,1)} %param.8) | copy-start | bytes 1572868
  7.2 155.2 %all-gather.3.cloned.1.call-start = ((), (), s32[]{:S(2)}) async-start(), calls=%async_computation.4 | async-start | bytes 6488064 | tf_op jit(solution)/shard_map/all_gather | solution.py:16
  147.4 1.0 copy-start.2
  162.4 4.8 %copy-start.1 = (bf16[2048,1536]{1,0:T(8,128)(2,1)S(1)}, bf16[2048,1536]{1,0:T(8,128)(2,1)}, u32[]{:S(2)}) copy-start(bf16[2048,1536]{1,0:T(8,128)(2,1)} %all-gather.3.cloned.1.call-done) | copy-start | bytes 18874372
  256.3 20.2 %all-to-all-start.2 = ((f32[16,3,8,512]{3,2,1,0:T(8,128)}), f32[16,3,8,512]{3,2,1,0:T(8,128)S(1)}, u32[]{:S(2)}, u32[]{:S(2)}) async-start(f32[16,3,8,512]{3,2,1,0:T(8,128)} %broadcast_in_dim.9), calls=%async_computation.2 | async-start | bytes 1572864 | tf_op jit(solution)/shard_map/all_to_all | solution.py:31
  276.5 20.6 %copy-start.4 = (f32[3,8,512]{2,1,0:T(8,128)S(1)}, f32[3,8,512]{2,1,0:T(8,128)}, u32[]{:S(2)}) copy-start(f32[3,8,512]{2,1,0:T(8,128)} %param.15) | copy-start | bytes 147460
  276.5 20.6 %copy-start.5 = (f32[3,8,512]{2,1,0:T(8,128)S(1)}, f32[3,8,512]{2,1,0:T(8,128)}, u32[]{:S(2)}) copy-start(f32[3,8,512]{2,1,0:T(8,128)} %param.14) | copy-start | bytes 147460
  278.4 17.3 %all-to-all-start.3 = ((f32[32,1,1]{2,1,0:T(1,128)}), f32[32,1,1]{2,1,0:T(1,128)S(1)}, u32[]{:S(2)}, u32[]{:S(2)}) async-start(f32[32,1,1]{2,1,0:T(1,128)} %broadcast_in_dim.10), calls=%async_computation.3 | async-start | bytes 32768 | tf_op jit(solution)/shard_map/all_to_all | solution.py:31
  287.1 42.2 %copy-start.3 = (f32[64,256]{1,0:T(8,128)S(1)}, f32[64,256]{1,0:T(8,128)}, u32[]{:S(2)}) copy-start(f32[64,256]{1,0:T(8,128)} %param.13) | copy-start | bytes 196612
Sparse Core Ops, SparseCore 0:
  10.7 151.6 all-gather.2
where the time goes:
time: 338 us; the launch traced here: 337 us
  blocking collectives  254 us (75%)
  waiting for transfers between devices  32.3 us (10%)
  matrix products  15.2 us (4%)
  between operations  14.9 us (4%)
  starting transfers between devices  12.3 us (4%)
  local copies, waits for them, and re-layouts  4.19 us (1%)
  other arithmetic  4.12 us (1%)
    all_to_all x1, blocking collectives, copy_for_each(): lax.all_to_all(jnp.broadcast_to(value[None], (peers, *value.shape)), axis...  137 us
    all_to_all x1, blocking collectives, sum_at_owner(): lax.all_to_all(pieces, axis, split_axis=0, concat_axis=0, tiled=True)  85.5 us
    all_gather x2, blocking collectives, gather_in_order(): pieces = lax.all_gather(pieces, axes[k], axis=0, tiled=True)  31.4 us
    all_to_all x2, waiting for transfers between devices, copy_for_each(): lax.all_to_all(jnp.broadcast_to(value[None], (peers, *value.shape)), axis...  19.6 us
    all_gather x1, waiting for transfers between devices, in_one_piece(): lax.all_gather(both, axis, axis=dim, tiled=True)  12.7 us
    all_to_all x2, starting transfers between devices, copy_for_each(): lax.all_to_all(jnp.broadcast_to(value[None], (peers, *value.shape)), axis...  12.3 us
  transfers between devices with their start and end apart: 3, of which 3 were waited for; matrix products, arithmetic and copies ran while one was open for 2% of the time, Pallas kernels for 0%

commit v1 on v0

--- a/solution.py
+++ b/solution.py
@@ -55,7 +55,9 @@
 def gather_in_order(value, axes, order):
     pieces = value[None]
     for k in order:
-        pieces = lax.all_gather(pieces, axes[k], axis=0, tiled=True)
+        pieces = jnp.concatenate(
+            lax.all_to_all(jnp.stack([pieces] * lax.axis_size(axes[k])), axes[k], 0, 0), axis=0
+        )
     block = [lax.axis_size(axes[k]) for k in reversed(order)]
     pieces = pieces.reshape(*block, *value.shape)
     turned = sorted(range(len(order)), key=lambda place: order[len(order) - 1 - place])

time: 338 us -> 337 us (level)
  blocking collectives: 254 us -> 270 us
  starting transfers between devices: 12.3 us -> 3.59 us
  waiting for transfers between devices: 32.3 us -> 24.9 us
    all_to_all x1 -> x3, blocking collectives: 137 us -> 174 us  [copy_for_each(): lax.all_to_all(jnp.broadcast_to(value[None], (peers, *value.shape)), axis...]
    all_gather x2 -> x0, blocking collectives: 31.4 us -> none  [gather_in_order(): pieces = lax.all_gather(pieces, axes[k], axis=0, tiled=True)]
    all_to_all x0 -> x1, blocking collectives: none -> 10.9 us  [gather_in_order(): lax.all_to_all(jnp.stack([pieces] * lax.axis_size(axes[k])), axes[k], 0, 0)]
    all_to_all x2 -> x1, starting transfers between devices: 12.3 us -> 3.55 us  [gather_in_order(): lax.all_to_all(jnp.stack([pieces] * lax.axis_size(axes[k])), axes[k], 0, 0)]
    all_to_all x2 -> x1, waiting for transfers between devices: 19.6 us -> 12.3 us  [gather_in_order(): lax.all_to_all(jnp.stack([pieces] * lax.axis_size(axes[k])), axes[k], 0, 0)]
  transfers between devices with their start and end apart: 3 -> 2, of which waited for: 3 -> 2; matrix products, arithmetic and copies ran while one was open for 2% -> 2% of each run, Pallas kernels for 0% -> 0%
where the time goes in v1:
time: 337 us
  blocking collectives  270 us (80%)
  waiting for transfers between devices  24.9 us (7%)
  matrix products  15.2 us (5%)
  between operations  14.9 us (4%)
  other arithmetic  4.17 us (1%)
  starting transfers between devices  3.59 us (1%)
  local copies, waits for them, and re-layouts  3.52 us (1%)
    all_to_all x3, blocking collectives, copy_for_each(): lax.all_to_all(jnp.broadcast_to(value[None], (peers, *value.shape)), axis...  174 us
    all_to_all x1, blocking collectives, sum_at_owner(): lax.all_to_all(pieces, axis, split_axis=0, concat_axis=0, tiled=True)  85.5 us
    all_gather x1, waiting for transfers between devices, in_one_piece(): lax.all_gather(both, axis, axis=dim, tiled=True)  12.7 us
    all_to_all x1, waiting for transfers between devices, gather_in_order(): lax.all_to_all(jnp.stack([pieces] * lax.axis_size(axes[k])), axes[k], 0, 0)  12.3 us
    all_to_all x1, blocking collectives, gather_in_order(): lax.all_to_all(jnp.stack([pieces] * lax.axis_size(axes[k])), axes[k], 0, 0)  10.9 us
  transfers between devices with their start and end apart: 2, of which 2 were waited for; matrix products, arithmetic and copies ran while one was open for 2% of the time, Pallas kernels for 0%

profile of v1, /device:TPU:1, one launch (start us, length us, event | category | flops | bytes accessed | tf_op | source)
XLA Modules:
  0.0 336.6 jit_solution(4547234676168937089)
XLA Ops:
  7.2 1.6 pad_maximum_fusion.1
  8.9 1.1 broadcast_in_dim.6
  10.0 137.4 %all_to_all.31 = f32[32,64,256]{2,1,0:T(8,128)S(1)} all-to-all(f32[32,64,256]{2,1,0:T(8,128)S(1)} %broadcast_in_dim.6), channel_id=1, replica_groups=mesh['group'=16,'member_0'=16,'member_1'=2] {'member_0','member_1'}, dimensions={0} | all-to-all | bytes 4194304 | tf_op jit(solution)/shard_map/all_to_all | solution.py:31
  147.7 0.8 copy-done.2
  149.1 0.3 fusion.24
  149.4 0.3 fusion.23
  149.8 12.7 %all-gather.2.cloned.1.call-done = bf16[2048,1536]{1,0:T(8,128)(2,1)} async-done(((bf16[64,1536]{1,0:T(8,128)(2,1)}), bf16[2048,1536]{1,0:T(8,128)(2,1)}) %all-gather.2.cloned.1.call-update) | async-done | bytes 6291472 | tf_op jit(solution)/shard_map/all_gather | solution.py:16
  162.4 2.5 fusion.17
  164.9 2.3 fusion.20
  167.3 0.8 multiply_convert_fusion
  169.7 85.5 %all_to_all.32 = f32[32,3,8,512]{3,2,1,0:T(8,128)S(1)} all-to-all(f32[32,3,8,512]{3,2,1,0:T(8,128)S(1)} %maximum_bitcast_fusion), channel_id=1, replica_groups=mesh['group'=16,'member_0'=16,'member_1'=2] {'member_0','member_1'}, dimensions={0} | all-to-all | bytes 3145728 | tf_op jit(solution)/shard_map/all_to_all | solution.py:47
  255.4 20.2 %all_to_all.33 = f32[16,3,8,512]{3,2,1,0:T(8,128)S(1)} all-to-all(f32[16,3,8,512]{3,2,1,0:T(8,128)S(1)} %broadcast_in_dim.7), channel_id=1, replica_groups=mesh['group'=16,'member_0'=16,'member_1'=2] {'group'}, dimensions={0} | all-to-all | bytes 1572864 | tf_op jit(solution)/shard_map/all_to_all | solution.py:31
  275.7 0.6 multiply_reduce_fusion
  276.3 0.7 broadcast_in_dim.8
  277.0 16.1 %all_to_all.34 = f32[32,1,1]{2,1,0:T(1,128)S(1)} all-to-all(f32[32,1,1]{2,1,0:T(1,128)S(1)} %broadcast_in_dim.8), channel_id=1, replica_groups=mesh['group'=16,'member_0'=16,'member_1'=2] {'member_0','member_1'}, dimensions={0} | all-to-all | bytes 256 | tf_op jit(solution)/shard_map/all_to_all | solution.py:31
  293.1 0.6 reduce_sum.39
  294.5 0.7 divide_convert_fusion
  295.1 0.8 stack.22
  295.9 3.6 %all-to-all-start.4 = ((bf16[16,1,3,8,512]{4,3,2,1,0:T(8,128)(2,1)}), bf16[16,1,3,8,512]{4,3,2,1,0:T(8,128)(2,1)S(1)}, u32[]{:S(2)}, u32[]{:S(2)}) async-start(bf16[16,1,3,8,512]{4,3,2,1,0:T(8,128)(2,1)} %stack.22), calls=%async_computation.4 | async-start | bytes 786432 | tf_op jit(solution)/shard_map/all_to_all | solution.py:59
  299.5 2.4 fusion.4
  301.9 3.2 fusion
  305.1 12.3 %all-to-all-done.4 = bf16[16,1,3,8,512]{4,3,2,1,0:T(8,128)(2,1)S(1)} async-done(((bf16[16,1,3,8,512]{4,3,2,1,0:T(8,128)(2,1)}), bf16[16,1,3,8,512]{4,3,2,1,0:T(8,128)(2,1)S(1)}, u32[]{:S(2)}, u32[]{:S(2)}) %all-to-all-start.4) | async-done | bytes 393248 | tf_op jit(solution)/shard_map/all_to_all | solution.py:59
  317.5 10.9 %all_to_all.35 = bf16[2,16,3,8,512]{4,3,1,2,0:T(8,128)(2,1)S(1)} all-to-all(bf16[2,16,3,8,512]{4,3,1,2,0:T(8,128)(2,1)S(1)} %copy.42), channel_id=1, replica_groups=mesh['group'=16,'member_0'=16,'member_1'=2] {'member_1'}, dimensions={0} | all-to-all | bytes 1572864 | tf_op jit(solution)/shard_map/all_to_all | solution.py:59
  328.5 1.3 convolution_bitcast_fusion
  (29 shorter events, 3.0 us)
Async XLA Ops:
  7.2 141.6 %copy-start = (bf16[128,2048]{1,0:T(8,128)(2,1)S(1)}, bf16[128,2048]{1,0:T(8,128)(2,1)}, u32[]{:S(2)}) copy-start(bf16[128,2048]{1,0:T(8,128)(2,1)} %param.8) | copy-start | bytes 1572868
  7.2 155.2 %all-gather.2.cloned.1.call-start = ((), (), s32[]{:S(2)}) async-start(), calls=%async_computation.6 | async-start | bytes 6488064 | tf_op jit(solution)/shard_map/all_gather | solution.py:16
  147.4 1.0 copy-start.2
  162.4 4.8 %copy-start.1 = (bf16[2048,1536]{1,0:T(8,128)(2,1)S(1)}, bf16[2048,1536]{1,0:T(8,128)(2,1)}, u32[]{:S(2)}) copy-start(bf16[2048,1536]{1,0:T(8,128)(2,1)} %all-gather.2.cloned.1.call-done) | copy-start | bytes 18874372
  255.2 39.2 %copy-start.4 = (f32[3,8,512]{2,1,0:T(8,128)S(1)}, f32[3,8,512]{2,1,0:T(8,128)}, u32[]{:S(2)}) copy-start(f32[3,8,512]{2,1,0:T(8,128)} %param.15) | copy-start | bytes 147460
  255.2 39.2 %copy-start.5 = (f32[3,8,512]{2,1,0:T(8,128)S(1)}, f32[3,8,512]{2,1,0:T(8,128)}, u32[]{:S(2)}) copy-start(f32[3,8,512]{2,1,0:T(8,128)} %param.14) | copy-start | bytes 147460
  295.9 21.5 %all-to-all-start.4 = ((bf16[16,1,3,8,512]{4,3,2,1,0:T(8,128)(2,1)}), bf16[16,1,3,8,512]{4,3,2,1,0:T(8,128)(2,1)S(1)}, u32[]{:S(2)}, u32[]{:S(2)}) async-start(bf16[16,1,3,8,512]{4,3,2,1,0:T(8,128)(2,1)} %stack.22), calls=%async_computation.4 | async-start | bytes 786432 | tf_op jit(solution)/shard_map/all_to_all | solution.py:59
  317.5 11.0 %copy-start.3 = (f32[64,256]{1,0:T(8,128)S(1)}, f32[64,256]{1,0:T(8,128)}, u32[]{:S(2)}) copy-start(f32[64,256]{1,0:T(8,128)} %param.13) | copy-start | bytes 196612
Sparse Core Ops, SparseCore 0:
  10.7 151.6 all-gather.1
